TPU v7x, 32 devices: a whole 2x2x4 slice. The times are simulated.
32 devices in a mesh: groups: 2 (over y), fsdp: 4 (over z), mp: 2 (over x), sub: 2 (over core).
Axes of the slice: x: 2, y: 2, z: 4, core: 2. Of those that a mesh axis runs over, the one named last changes fastest.
Arguments:
- hidden: bfloat16 [128, 36864], P(('groups', 'fsdp', 'sub'), 'mp'), parts along dimension 0, may hold values from -6 to 6
- residual: bfloat16 [128, 4608], P(('groups', 'fsdp', 'sub')), parts along dimension 0, may hold values from -6 to 6
- down_packed: int32 [4608, 4608], P('mp', 'fsdp'), may hold values from -2147483648 to 2147483646
- down_scale: bfloat16 [288, 4608], P('mp', 'fsdp'), may hold values from 0.00049972534 to 0.0019989014
- post_gain: float32 [4608], replicated, may hold values from 0.1 to 1.9
- final_gain: float32 [4608], replicated, may hold values from 0.1 to 1.9
- embed_packed: int32 [8192, 576], P(('fsdp', 'mp', 'sub')), may hold values from -2147483648 to 2147483646
- embed_scale: bfloat16 [8192, 36], P(('fsdp', 'mp', 'sub')), may hold values from 0.0059814453 to 0.029907227
- targets: int32 [128], P(('groups', 'fsdp', 'sub')), parts along dimension 0, may hold values from 0 to 8191
- loss_mask: int32 [128], P(('groups', 'fsdp', 'sub')), parts along dimension 0, may hold values 0 or 1
Outputs:
- token_loss: float32 [128], P(('groups', 'fsdp', 'sub')), parts along dimension 0
- mean_loss: float32 [2], P('groups'), parts along dimension 0
There are 2 independent parts, one for each index of `groups`. A program takes and returns all parts, laid end to end along the dimension named above; an argument that names none is the same for every part. Nothing has to cross between parts.
Inputs may be any that keep to these rules, and one draw needn't show every extreme that they name: `down_packed`: bits 4 k to 4 k + 3 of the word in row r hold the signed code of row 8 r + k of the down projection, k = 0..7. `embed_packed`: bits 4 k to 4 k + 3 of the word in column j hold the signed code of column k * 576 + j of the embedding, k = 0..7.
All inputs are finite; a program needn't handle non-finite values. No bound on the sum of `loss_mask` on one device may be relied on, other than what follows from the above.
Results may differ from a plain program's by a relative error of at most 0.00097.
Values may be sent and summed in bfloat16 or wider, within the bound.
A program may use at most 128 MiB of HBM per device.

v0:
```python
import jax
import jax.numpy as jnp
from jax import lax
from jax.sharding import PartitionSpec as P

EPS = 1e-06
CAP = 30.0


def signed_planes(words):
    shifts = (28 - 4 * jnp.arange(8, dtype=jnp.int32))[None, :, None]
    lifted = jnp.left_shift(words[:, None, :], shifts)
    return jnp.right_shift(lifted, 28)


def dequant_down(words, scales):
    cols = words.shape[1]
    codes = signed_planes(words).astype(jnp.bfloat16)
    grouped = codes.reshape(scales.shape[0], -1, cols) * scales[:, None, :]
    return grouped.reshape(-1, cols)


def dequant_embed(words, scales):
    rows = words.shape[0]
    codes = signed_planes(words).astype(jnp.bfloat16)
    grouped = codes.reshape(rows, scales.shape[1], -1) * scales[:, :, None]
    return grouped.reshape(rows, -1)


def normalize_rows(ffn, residual, post_gain, final_gain):
    ffn = lax.psum(ffn, "mp")
    normed = ffn * lax.rsqrt(jnp.mean(ffn * ffn, axis=-1, keepdims=True) + EPS) * post_gain
    stream = residual.astype(jnp.float32) + normed
    return (
        stream * lax.rsqrt(jnp.mean(stream * stream, axis=-1, keepdims=True) + EPS) * final_gain
    ).astype(jnp.bfloat16)


def on_device(
    hidden,
    residual,
    down_packed,
    down_scale,
    post_gain,
    final_gain,
    embed_packed,
    embed_scale,
    targets,
    loss_mask,
):
    tok_rows = hidden.shape[0]
    local_weight = dequant_down(down_packed, down_scale)
    partial_cols = jnp.dot(
        lax.all_gather(hidden, "fsdp", axis=0, tiled=True),
        local_weight,
        preferred_element_type=jnp.float32,
    )
    ffn = lax.all_to_all(partial_cols, "fsdp", split_axis=0, concat_axis=1, tiled=True)
    states = normalize_rows(ffn, residual, post_gain, final_gain)
    all_states, all_targets = (
        lax.all_gather(states, ("fsdp", "sub"), axis=0, tiled=True),
        lax.all_gather(targets, ("fsdp", "sub"), axis=0, tiled=True),
    )
    embed = dequant_embed(embed_packed, embed_scale)
    logits = lax.dot_general(
        all_states, embed, (((1,), (1,)), ((), ())), preferred_element_type=jnp.float32
    )
    capped = CAP * jnp.tanh(logits / CAP)
    vocab_rows = embed.shape[0]
    first_id = lax.axis_index(("fsdp", "mp", "sub")) * vocab_rows
    ids = first_id + jnp.arange(vocab_rows, dtype=jnp.int32)
    hits = all_targets[:, None] == ids[None, :]
    exp_sums, target_logits = lax.psum(
        (jnp.sum(jnp.exp(capped), axis=1), jnp.sum(jnp.where(hits, capped, 0.0), axis=1)),
        ("fsdp", "mp", "sub"),
    )
    own_start = lax.axis_index(("fsdp", "sub")) * tok_rows
    own_sums = lax.dynamic_slice_in_dim(exp_sums, own_start, tok_rows, 0)
    own_targets = lax.dynamic_slice_in_dim(target_logits, own_start, tok_rows, 0)
    weights = loss_mask.astype(jnp.float32)
    token_loss = weights * (jnp.log(own_sums) - own_targets)
    loss_sum, count = lax.psum((jnp.sum(token_loss), jnp.sum(weights)), ("fsdp", "sub"))
    mean_loss = (loss_sum / jnp.maximum(count, 1.0)).reshape(1)
    return (token_loss, mean_loss)


def solution(mesh):
    return jax.shard_map(
        on_device,
        mesh=mesh,
        in_specs=(
            P(("groups", "fsdp", "sub"), "mp"),
            P(("groups", "fsdp", "sub"), None),
            P("mp", "fsdp"),
            P("mp", "fsdp"),
            P(),
            P(),
            P(("fsdp", "mp", "sub"), None),
            P(("fsdp", "mp", "sub"), None),
            P(("groups", "fsdp", "sub")),
            P(("groups", "fsdp", "sub")),
        ),
        out_specs=(P(("groups", "fsdp", "sub")), P("groups")),
        check_vma=False,
    )
```

profile of v0, /device:TPU:0, one launch (start us, length us, event | category | flops | bytes accessed | tf_op | source)
XLA Modules:
  0.0 167.8 jit_solution(12297695420085963303)
XLA Ops:
  7.2 0.0 all-gather.2.cloned.1.call-start
  7.2 0.7 all-gather.2.cloned.1.call-update
  7.9 0.0 all-reduce.5.cloned.1.call-start
  8.0 0.1 shift_left.49
  8.1 17.8 %fusion.2 = bf16[18432,1152]{1,0:T(8,128)(2,1)} fusion(s32[18432]{0:T(1024)S(1)} %broadcast_bitcast_fusion, s32[2304,1152]{1,0:T(8,128)} %param.12, bf16[144,1152]{1,0:T(8,128)(2,1)} %param.13), kind=kLoop, calls=%fused_computation.3 | loop fusion | flops 148635648 | bytes 53489664 | tf_op jit(solution)/shard_map/mul | solution.py:19
  25.9 0.0 copy-start.7
  25.9 0.0 copy-start.6
  25.9 0.0 copy-start
  25.9 0.0 copy-start.3
  26.0 0.0 copy-start.1
  26.0 0.0 copy-start.2
  26.0 0.0 copy-start.4
  26.0 16.6 %all-gather.2.cloned.1.call-done = bf16[32,18432]{1,0:T(8,128)(2,1)} async-done(((bf16[8,18432]{1,0:T(8,128)(2,1)}), bf16[32,18432]{1,0:T(8,128)(2,1)}) %all-gather.2.cloned.1.call-update) | async-done | bytes 1179664 | tf_op jit(solution)/shard_map/all_gather | solution.py:54
  42.6 15.8 %convolution_bitcast_fusion = f32[4,8,1152]{2,1,0:T(8,128)S(1)} fusion(bf16[32,18432]{1,0:T(8,128)(2,1)} %all-gather.2.cloned.1.call-done, bf16[18432,1152]{1,0:T(8,128)(2,1)} %fusion.2), kind=kOutput, calls=%fused_computation.8 | convolution fusion | flops 1358954496 | bytes 43794432 | tf_op jit(solution)/shard_map/dot_general | solution.py:53
  58.4 0.0 copy-start.5
  58.4 9.7 %all_to_all.19 = f32[4,8,1152]{2,1,0:T(8,128)} all-to-all(f32[4,8,1152]{2,1,0:T(8,128)S(1)} %convolution_bitcast_fusion), channel_id=1, replica_groups=mesh['groups'=2,'fsdp'=4,'mp'=2,'sub'=2] {'fsdp'}, dimensions={0} | all-to-all | bytes 294912 | tf_op jit(solution)/shard_map/all_to_all | solution.py:58
  68.1 0.0 all-reduce.5.cloned.1.call-update
  68.1 0.1 shift_left.56
  68.2 0.1 shift_left.57
  68.3 0.6 dynamic-slice
  69.5 0.2 dynamic-update-slice
  69.8 3.6 %fusion.5 = bf16[512,4608]{0,1:T(8,128)(2,1)} fusion(s32[4608]{0:T(1024)S(1)} %shift_left.57, s32[512,576]{0,1:T(8,128)S(1)} %copy-done, bf16[512,36]{0,1:T(8,128)(2,1)S(1)} %copy-done.3), kind=kLoop, calls=%fused_computation.7 | loop fusion | flops 16515072 | bytes 5953536 | tf_op jit(solution)/shard_map/mul | solution.py:26
  73.4 6.5 %all-reduce = s32[64]{0:T(128)S(1)} all-reduce(s32[64]{0:T(128)S(1)} %dynamic-update-slice), channel_id=1, replica_groups=mesh['groups'=2,'fsdp'=4,'mp'=2,'sub'=2] {'fsdp','sub'}, use_global_device_ids=true, to_apply=%add | all-reduce | flops 64 | bytes 512
  79.8 8.8 %all-reduce.5.cloned.1.call-done = f32[8,4608]{1,0:T(8,128)} async-done(((f32[8,4608]{1,0:T(8,128)}), f32[8,4608]{1,0:T(8,128)}) %all-reduce.5.cloned.1.call-update) | async-done | bytes 147472 | tf_op jit(solution)/shard_map/psum | solution.py:31
  88.7 1.1 multiply_reduce_fusion.1
  89.8 1.1 multiply_reduce_fusion
  90.9 1.0 multiply_convert_fusion
  91.9 15.1 %all_gather.10 = bf16[64,4608]{1,0:T(8,128)(2,1)S(1)} all-gather(bf16[8,4608]{1,0:T(8,128)(2,1)S(1)} %multiply_convert_fusion), channel_id=1, replica_groups=mesh['groups'=2,'fsdp'=4,'mp'=2,'sub'=2] {'fsdp','sub'}, dimensions={0}, use_global_device_ids=true | all-gather | bytes 663552 | tf_op jit(solution)/shard_map/all_gather | solution.py:61
  107.0 3.4 %exponential_reduce_fusion = (f32[64]{0:T(128)S(1)}, f32[64]{0:T(128)S(1)}) fusion(s32[512]{0:T(512)S(1)} %iota_add_fusion, s32[64]{0:T(128)S(1)} %all-reduce, bf16[64,4608]{1,0:T(8,128)(2,1)S(1)} %all_gather.10, bf16[512,4608]{0,1:T(8,128)(2,1)} %fusion.5), kind=kOutput, calls=%fused_computation.17 | convolution fusion | flops 302186368 | bytes 5311232 | tf_op jit(solution)/shard_map/dot_general | solution.py:65
  110.4 32.7 %all-reduce.1 = (f32[64]{0:T(128)S(1)}, f32[64]{0:T(128)S(1)}) all-reduce(f32[64]{0:T(128)S(1)} %get-tuple-element.3, f32[64]{0:T(128)S(1)} %get-tuple-element.2), channel_id=1, replica_groups=mesh['groups'=2,'fsdp'=4,'mp'=2,'sub'=2] {'fsdp','mp','sub'}, use_global_device_ids=true, to_apply=%region_6.7 | all-reduce | flops 128 | bytes 1024 | tf_op jit(solution)/shard_map/psum | solution.py:73
  143.1 1.3 fusion.8
  144.4 14.2 %all-reduce.2 = (f32[]{:T(128)}, f32[]{:T(128)}) all-reduce(f32[]{:T(128)} %get-tuple-element.8, f32[]{:T(128)} %get-tuple-element.10), channel_id=1, replica_groups=mesh['groups'=2,'fsdp'=4,'mp'=2,'sub'=2] {'fsdp','sub'}, use_global_device_ids=true, to_apply=%region_8.9 | all-reduce | flops 2 | bytes 16 | tf_op jit(solution)/shard_map/psum | solution.py:82
  (15 shorter events, 0.1 us)
Async XLA Ops:
  7.2 35.4 %all-gather.2.cloned.1.call-start = ((), (), s32[]{:S(2)}) async-start(), calls=%async_computation.1 | async-start | bytes 1474560 | tf_op jit(solution)/shard_map/all_gather | solution.py:54
  7.9 80.8 %all-reduce.5.cloned.1.call-start = ((), (), s32[]{:S(2)}) async-start(), calls=%async_computation.2 | async-start | bytes 294912 | tf_op jit(solution)/shard_map/psum | solution.py:31
  25.9 42.4 %copy-start.7 = (u32[32]{0:T(128)S(1)}, u32[32]{0:T(128)}, u32[]{:S(2)}) copy-start(u32[32]{0:T(128)} %constant.48) | copy-start | bytes 388
  25.9 43.6 %copy-start.6 = (s32[8]{0:T(128)S(1)}, s32[8]{0:T(128)}, u32[]{:S(2)}) copy-start(s32[8]{0:T(128)} %param.18) | copy-start | bytes 100
  25.9 43.9 %copy-start = (s32[512,576]{0,1:T(8,128)S(1)}, s32[512,576]{0,1:T(8,128)}, u32[]{:S(2)}) copy-start(s32[512,576]{0,1:T(8,128)} %param.16) | copy-start | bytes 3538948
  25.9 43.8 %copy-start.3 = (bf16[512,36]{0,1:T(8,128)(2,1)S(1)}, bf16[512,36]{0,1:T(8,128)(2,1)}, u32[]{:S(2)}) copy-start(bf16[512,36]{0,1:T(8,128)(2,1)} %param.17) | copy-start | bytes 110596
  26.0 63.8 %copy-start.1 = (bf16[8,4608]{1,0:T(8,128)(2,1)S(1)}, bf16[8,4608]{1,0:T(8,128)(2,1)}, u32[]{:S(2)}) copy-start(bf16[8,4608]{1,0:T(8,128)(2,1)} %param.11) | copy-start | bytes 221188
  26.0 63.8 %copy-start.2 = (f32[4608]{0:T(1024)S(1)}, f32[4608]{0:T(1024)}, u32[]{:S(2)}) copy-start(f32[4608]{0:T(1024)} %param.14) | copy-start | bytes 55300
  26.0 64.9 %copy-start.4 = (f32[4608]{0:T(1024)S(1)}, f32[4608]{0:T(1024)}, u32[]{:S(2)}) copy-start(f32[4608]{0:T(1024)} %param.15) | copy-start | bytes 55300
  58.4 84.8 %copy-start.5 = (s32[8]{0:T(128)S(1)}, s32[8]{0:T(128)}, u32[]{:S(2)}) copy-start(s32[8]{0:T(128)} %param.19) | copy-start | bytes 100
Sparse Core Ops, SparseCore 0:
  9.5 32.9 all-gather.1
  68.2 20.3 all-reduce.4
where the time goes:
time: 168 us
  blocking collectives  78.2 us (47%)
  waiting for transfers between devices  26.1 us (16%)
  other arithmetic  25.9 us (15%)
  matrix products  19.2 us (11%)
  between operations  17.2 us (10%)
    psum x1, blocking collectives, on_device(): lax.psum((jnp.sum(jnp.exp(capped), axis=1), jnp.sum(jnp.where(hits, cappe...  32.7 us
    mul x1, other arithmetic, dequant_down(): grouped = codes.reshape(scales.shape[0], -1, cols) * scales[:, None, :]  17.8 us
    all_gather x1, waiting for transfers between devices, on_device(): lax.all_gather(hidden, 'fsdp', axis=0, tiled=True)  16.6 us
    dot_general x1, matrix products, on_device(): jnp.dot(lax.all_gather(hidden, 'fsdp', axis=0, tiled=True), local_weight,...  15.8 us
    all_gather x1, blocking collectives, on_device(): lax.all_gather(states, ('fsdp', 'sub'), axis=0, tiled=True)  15.1 us
    psum x1, blocking collectives, on_device(): lax.psum((jnp.sum(token_loss), jnp.sum(weights)), ('fsdp', 'sub'))  14.2 us
    all_to_all x1, blocking collectives, on_device(): lax.all_to_all(partial_cols, 'fsdp', split_axis=0, concat_axis=1, tiled=T...  9.71 us
    psum x1, waiting for transfers between devices, normalize_rows(): ffn = lax.psum(ffn, 'mp')  8.84 us
  transfers between devices with their start and end apart: 2, of which 2 were waited for; matrix products, arithmetic and copies ran while one was open for 13% of the time, Pallas kernels for 0%

commit v1 on v0

v1 whole, which is shorter than its diff:
```python
import functools

import jax
import jax.numpy as jnp
from jax import lax
from jax.experimental import pallas as pl
from jax.experimental.pallas import tpu as pltpu
from jax.sharding import PartitionSpec as P

EPS = 1e-06
CAP = 30.0
MESH = pl.DeviceIdType.MESH
PLANES = 8
EARLY = 0.6


def remote(src, dst, send, recv, f, m, s):
    return pltpu.make_async_remote_copy(
        src_ref=src,
        dst_ref=dst,
        send_sem=send,
        recv_sem=recv,
        device_id={"fsdp": f, "mp": m, "sub": s},
        device_id_type=MESH,
    )


def kernel(
    nf, nm, hidden, residual, words_hbm, scale, post_gain, final_gain, embed_hbm, embed_scale, info,
    out, words, scale_f, weight, perm, pair, gathered, own_acc, acc_in, mid, mid_in, red, cols_in,
    embed_words, embed, states, infos, sums,
    local_sem, pair_send, pair_recv, ring_send, ring_recv, info_send, info_recv,
    acc_sem, mid_send, mid_recv, col_send, col_recv, st_send, st_recv, fwd_send, fwd_recv,
    sum_send, sum_recv,
):
    f, m, s = lax.axis_index("fsdp"), lax.axis_index("mp"), lax.axis_index("sub")
    n = nf * nm * 2
    me = (f * nm + m) * 2 + s
    tok = hidden.shape[0]
    half_rows, cols = words.shape
    half_k = half_rows * PLANES
    total = tok * 2 * nf

    def where_is(q):
        return q // (2 * nm), (q // 2) % nm, q % 2

    load_words = pltpu.make_async_copy(
        words_hbm.at[pl.ds(pl.multiple_of(s * half_rows, 8), half_rows)], words, local_sem.at[0]
    )
    load_words.start()
    load_embed = pltpu.make_async_copy(embed_hbm, embed_words, local_sem.at[1])
    load_embed.start()

    barrier = pltpu.get_barrier_semaphore()
    for d in range(1, n):
        pf, pm, ps = where_is(lax.rem(me + d, n))
        pl.semaphore_signal(
            barrier, inc=1, device_id={"fsdp": pf, "mp": pm, "sub": ps}, device_id_type=MESH
        )

    width = perm.shape[0]
    q = width // PLANES
    step_rows = 128 if width % 128 == 0 else width

    def build(i, carry):
        start = pl.multiple_of(i * step_rows, step_rows)
        row = lax.broadcasted_iota(jnp.int32, (step_rows, width), 0) + start
        col = lax.broadcasted_iota(jnp.int32, (step_rows, width), 1)
        plane = sum(((col >= q * k).astype(jnp.int32) for k in range(1, PLANES)), jnp.zeros_like(col))
        source = (col - plane * q) * PLANES + plane
        perm[pl.ds(start, step_rows), :] = jnp.where(row == source, 1.0, 0.0).astype(jnp.bfloat16)
        return carry

    lax.fori_loop(0, width // step_rows, build, 0)
    scale_f[...] = scale[...].astype(jnp.float32)
    pair[s] = hidden[:, pl.ds(pl.multiple_of(s * half_k, 128), half_k)]
    infos[me] = info[...]

    pl.semaphore_wait(barrier, n - 1)

    swap = remote(
        hidden.at[:, pl.ds(pl.multiple_of((1 - s) * half_k, 128), half_k)],
        pair.at[s], pair_send, pair_recv, f, m, 1 - s,
    )
    swap.start()
    swap.wait_recv()

    both = pair[...].astype(jnp.float32).reshape(2 * tok, half_k)
    chunks = half_k // width
    stacked = jnp.concatenate(
        [both[:, c * width:(c + 1) * width] for c in range(chunks)], axis=0
    ).astype(jnp.bfloat16)
    ordered = jnp.dot(stacked, perm[...], preferred_element_type=jnp.float32).astype(jnp.bfloat16)
    for c in range(chunks):
        for k in range(PLANES):
            gathered[f, k, :, c * q:(c + 1) * q] = ordered[
                c * 2 * tok:(c + 1) * 2 * tok, k * q:(k + 1) * q
            ]

    far = nf // 2
    low, high = list(range(4)), list(range(4, 8))
    orders = (low + high, high + low)
    last = (low, high)
    pending = []
    waited = set()

    def block_at(way, j):
        return lax.rem(f - j + nf, nf) if way == 0 else lax.rem(f + j, nf)

    def hop(way, j, p):
        slot = block_at(way, j - 1)
        target = lax.rem(f + 1, nf) if way == 0 else lax.rem(f + nf - 1, nf)
        return remote(
            gathered.at[slot, p], gathered.at[slot, p], ring_send.at[way, j - 1, p],
            ring_recv.at[slot, p], target, m, s,
        )

    def send_hop(way, j, p):
        if j < far or p in last[way]:
            copy = hop(way, j, p)
            copy.start()
            pending.append(copy)

    def arrive(way, j, p):
        if (way, j, p) in waited or not (j < far or p in last[way]):
            return
        waited.add((way, j, p))
        slot = block_at(way, j)
        remote(
            gathered.at[slot, p], gathered.at[slot, p], ring_send.at[way, j - 1, p],
            ring_recv.at[slot, p], f, m, 1 - s,
        ).wait_recv()

    if nf > 1:
        for i in range(PLANES):
            for way in (0, 1):
                send_hop(way, 1, orders[way][i])

    for d in range(1, n):
        peer = lax.rem(me + d, n)
        pf, pm, ps = where_is(peer)
        copy = remote(info, infos.at[me], info_send.at[d], info_recv.at[me], pf, pm, ps)
        copy.start()
        pending.append(copy)

    load_words.wait()
    per = half_rows // (scale.shape[0] // 2)
    groups = half_rows // per

    def dequant(i, carry):
        start = pl.multiple_of(i * per, per)
        w = words[pl.ds(start, per), :]
        sc = scale_f[pl.ds(s * groups + i, 1), :]
        for k in range(PLANES):
            code = jnp.right_shift(jnp.left_shift(w, 28 - 4 * k), 28) if k < 7 else jnp.right_shift(w, 28)
            weight[k, pl.ds(start, per), :] = (code.astype(jnp.float32) * sc).astype(jnp.bfloat16)
        return carry

    early = int(groups * EARLY)
    lax.fori_loop(0, early, dequant, 0)
    for j in range(1, far):
        for i in range(PLANES):
            for way in (0, 1):
                p = orders[way][i]
                if j + 1 < far or p in last[way]:
                    arrive(way, j, p)
                    send_hop(way, j + 1, p)
    lax.fori_loop(early, groups, dequant, 0)

    load_embed.wait()
    vocab, packed = embed_words.shape
    erows = 32
    tiles = 2 * packed // 128

    def dequant_embed(i, carry):
        start = pl.multiple_of(i * erows, erows)
        w = embed_words[pl.ds(start, erows), :]
        side = jnp.concatenate([w, w], axis=1)
        es = embed_scale[pl.ds(start, erows), :].astype(jnp.float32)
        lane = lax.broadcasted_iota(jnp.int32, (erows, 128), 1)
        for kk in range(PLANES // 2):
            for t in range(tiles):
                x = side[:, t * 128:(t + 1) * 128]
                a = 28 - 8 * kk
                if (t + 1) * 128 <= packed:
                    x = jnp.left_shift(x, a)
                elif t * 128 >= packed:
                    x = jnp.left_shift(x, a - 4)
                else:
                    x = jnp.left_shift(x, jnp.where(lane < packed - t * 128, a, a - 4))
                g = kk * tiles + t
                embed[pl.ds(start, erows), g * 128:(g + 1) * 128] = (
                    jnp.right_shift(x, 28).astype(jnp.float32) * es[:, g:g + 1]
                ).astype(jnp.bfloat16)
        return carry

    lax.fori_loop(0, vocab // erows, dequant_embed, 0)

    acc = jnp.zeros((total, cols), jnp.float32)
    for p in (0, 4, 1, 5, 2, 6, 3, 7):
        for j in range(1, far + 1):
            for way in (0, 1):
                arrive(way, j, p)
        lhs = gathered[:, p].reshape(total, half_rows)
        acc = acc + jnp.dot(lhs, weight[p], preferred_element_type=jnp.float32)

    for b in range(nf):
        for h in (0, 1):
            r = (2 * b + h) * tok
            own_acc[h, b] = acc[r:r + tok]

    swap_acc = remote(own_acc.at[1 - s], acc_in, acc_sem.at[0], acc_sem.at[1], f, m, 1 - s)
    swap_acc.start()
    swap_acc.wait_recv()
    for b in range(nf):
        mid[b % nm, b // nm] = own_acc[s, b] + acc_in[b]
    for d in range(1, nm):
        pm = lax.rem(m + d, nm)
        copy = remote(mid.at[pm], mid_in.at[m], mid_send.at[d], mid_recv.at[m], f, pm, s)
        copy.start()
        pending.append(copy)
    part = mid[m]
    for d in range(1, nm):
        pm = lax.rem(m + d, nm)
        remote(mid.at[m], mid_in.at[pm], mid_send.at[0], mid_recv.at[pm], f, pm, s).wait_recv()
        part = part + mid_in[pm]
    red[...] = part

    def to_owner(j):
        target = j * nm + m
        return target, remote(
            red.at[j], cols_in.at[f], col_send.at[j], col_recv.at[f], target, m, s
        )

    for j in range(nf // nm):
        target, copy = to_owner(j)

        @pl.when(target != f)
        def _():
            copy.start()

        @pl.when(target == f)
        def _():
            cols_in[f] = red[j]

    owner = lax.rem(f, nm) == m

    def state_sends():
        copies = []
        for df in range(nf):
            for dm in range(nm):
                if df or dm:
                    copies.append(remote(
                        states.at[f, s], states.at[f, s], st_send.at[df * nm + dm], st_recv.at[f],
                        lax.rem(f + df, nf), lax.rem(m + dm, nm), s,
                    ))
        return copies

    width_d = nf * cols

    @pl.when(owner)
    def _():
        for d in range(1, nf):
            src = lax.rem(f + d, nf)
            remote(
                red.at[0], cols_in.at[src], col_send.at[0], col_recv.at[src], src, m, s
            ).wait_recv()
        ffn = jnp.concatenate([cols_in[b] for b in range(nf)], axis=1)
        inv = lax.rsqrt(jnp.sum(ffn * ffn, axis=1, keepdims=True) / width_d + EPS)
        stream = residual[...].astype(jnp.float32) + ffn * inv * post_gain[...]
        inv2 = lax.rsqrt(jnp.sum(stream * stream, axis=1, keepdims=True) / width_d + EPS)
        states[f, s] = (stream * inv2 * final_gain[...]).astype(jnp.bfloat16)
        for copy in state_sends():
            copy.start()

    def forward(b):
        return remote(
            states.at[b, s], states.at[b, s], fwd_send.at[b], fwd_recv.at[b], f, m, 1 - s
        )

    for d in range(nf):
        b = lax.rem(f + d, nf)
        got = remote(
            states.at[b, s], states.at[b, s], st_send.at[0], st_recv.at[b], f, m, 1 - s
        )
        if d == 0:
            @pl.when(jnp.logical_not(owner))
            def _():
                got.wait_recv()
        else:
            got.wait_recv()
        copy = forward(b)
        copy.start()
        pending.append(copy)
    for b in range(nf):
        remote(
            states.at[b, 1 - s], states.at[b, 1 - s], fwd_send.at[b], fwd_recv.at[b], f, m, 1 - s
        ).wait_recv()
    for d in range(1, n):
        src = lax.rem(me + n - d, n)
        remote(
            info, infos.at[src], info_send.at[d], info_recv.at[src], f, m, 1 - s
        ).wait_recv()

    all_states = states[...].astype(jnp.float32).reshape(total, width_d).astype(jnp.bfloat16)
    logits = lax.dot_general(
        all_states, embed[...], (((1,), (1,)), ((), ())), preferred_element_type=jnp.float32
    )
    capped = CAP * jnp.tanh(logits / CAP)
    rows = jnp.concatenate(
        [infos[b * nm * 2 + h] for b in range(nf) for h in (0, 1)], axis=0
    )
    ids = me * vocab + lax.broadcasted_iota(jnp.int32, (total, vocab), 1)
    hits = rows[:, 0:1] == ids
    e = jnp.sum(jnp.exp(capped), axis=1, keepdims=True)
    t = jnp.sum(jnp.where(hits, capped, 0.0), axis=1, keepdims=True)
    counted = rows[:, 64:65].astype(jnp.float32)
    lane = lax.broadcasted_iota(jnp.int32, (total, 128), 1)
    table = jnp.where(lane == 0, e, jnp.where(lane == 1, t, jnp.where(lane == 2, counted, 0.0)))
    pad = sums.shape[2]
    if pad > total:
        table = jnp.concatenate([table, jnp.zeros((pad - total, 128), jnp.float32)], axis=0)
    mine = jnp.transpose(table)[0:8, :]
    sums[me] = mine
    for d in range(1, n):
        pf, pm, ps = where_is(lax.rem(me + d, n))
        copy = remote(sums.at[me], sums.at[me], sum_send.at[d], sum_recv.at[me], pf, pm, ps)
        copy.start()
        pending.append(copy)
    for d in range(1, n):
        src = lax.rem(me + n - d, n)
        remote(
            sums.at[src], sums.at[src], sum_send.at[d], sum_recv.at[src], f, m, 1 - s
        ).wait_recv()
    added = jnp.sum(sums[...], axis=0)
    weights = mine[2:3, :]
    spot = lax.broadcasted_iota(jnp.int32, (1, pad), 1)
    exp_sums = jnp.where(spot < total, added[0:1, :], 1.0)
    losses = weights * (jnp.log(exp_sums) - added[1:2, :])
    mean = jnp.sum(losses, axis=1, keepdims=True) / jnp.maximum(
        jnp.sum(weights, axis=1, keepdims=True), 1.0
    )
    row = lax.broadcasted_iota(jnp.int32, (8, pad), 0)
    out[...] = jnp.where(row == 0, losses, mean)

    swap.wait_send()
    swap_acc.wait_send()
    for copy in pending:
        copy.wait_send()
    for j in range(nf // nm):
        target, copy = to_owner(j)

        @pl.when(target != f)
        def _():
            copy.wait_send()

    @pl.when(owner)
    def _():
        for copy in state_sends():
            copy.wait_send()


def on_device(
    nf, nm, hidden, residual, down_packed, down_scale, post_gain, final_gain, embed_packed, embed_scale,
    targets, loss_mask,
):
    tok, width_d = residual.shape
    rows, cols = down_packed.shape
    vocab, packed = embed_packed.shape
    half = rows // 2
    n = nf * nm * 2
    total = tok * 2 * nf
    pad = -(-total // 128) * 128
    chunk = PLANES * (128 if half % 128 == 0 else half)
    info = jnp.concatenate(
        [jnp.broadcast_to(targets[:, None], (tok, 64)), jnp.broadcast_to(loss_mask[:, None], (tok, 64))],
        axis=1,
    )
    vm = pl.BlockSpec(memory_space=pltpu.VMEM)
    hbm = pl.BlockSpec(memory_space=pl.ANY)
    dma = pltpu.SemaphoreType.DMA
    bf16, f32, i32 = jnp.bfloat16, jnp.float32, jnp.int32
    table = pl.pallas_call(
        functools.partial(kernel, nf, nm),
        out_shape=jax.ShapeDtypeStruct((8, pad), f32),
        in_specs=[vm, vm, hbm, vm, vm, vm, hbm, vm, vm],
        out_specs=vm,
        scratch_shapes=[
            pltpu.VMEM((half, cols), i32),
            pltpu.VMEM(down_scale.shape, f32),
            pltpu.VMEM((PLANES, half, cols), bf16),
            pltpu.VMEM((chunk, chunk), bf16),
            pltpu.VMEM((2, tok, half * PLANES), bf16),
            pltpu.VMEM((nf, PLANES, 2 * tok, half), bf16),
            pltpu.VMEM((2, nf, tok, cols), f32),
            pltpu.VMEM((nf, tok, cols), f32),
            pltpu.VMEM((nm, nf // nm, tok, cols), f32),
            pltpu.VMEM((nm, nf // nm, tok, cols), f32),
            pltpu.VMEM((nf // nm, tok, cols), f32),
            pltpu.VMEM((nf, tok, cols), f32),
            pltpu.VMEM((vocab, packed), i32),
            pltpu.VMEM((vocab, width_d), bf16),
            pltpu.VMEM((nf, 2, tok, width_d), bf16),
            pltpu.VMEM((n, tok, 128), i32),
            pltpu.VMEM((n, 8, pad), f32),
            dma((2,)),
            dma, dma,
            dma((2, max(nf // 2, 1), PLANES)), dma((nf, PLANES)),
            dma((n,)), dma((n,)),
            dma((2,)),
            dma((nm,)), dma((nm,)),
            dma((nf // nm,)), dma((nf,)),
            dma((nf * nm,)), dma((nf,)),
            dma((nf,)), dma((nf,)),
            dma((n,)), dma((n,)),
        ],
        compiler_params=pltpu.CompilerParams(
            collective_id=0, has_side_effects=True, vmem_limit_bytes=62 * 1024 * 1024
        ),
    )(
        hidden, residual, down_packed, down_scale, post_gain[None, :], final_gain[None, :],
        embed_packed, embed_scale, info,
    )
    start = (lax.axis_index("fsdp") * 2 + lax.axis_index("sub")) * tok
    return lax.dynamic_slice(table[0], (start,), (tok,)), table[1, 0:1]


def solution(mesh):
    nf, nm = mesh.shape["fsdp"], mesh.shape["mp"]
    return jax.shard_map(
        functools.partial(on_device, nf, nm),
        mesh=mesh,
        in_specs=(
            P(("groups", "fsdp", "sub"), "mp"),
            P(("groups", "fsdp", "sub"), None),
            P("mp", "fsdp"),
            P("mp", "fsdp"),
            P(),
            P(),
            P(("fsdp", "mp", "sub"), None),
            P(("fsdp", "mp", "sub"), None),
            P(("groups", "fsdp", "sub")),
            P(("groups", "fsdp", "sub")),
        ),
        out_specs=(P(("groups", "fsdp", "sub")), P("groups")),
        check_vma=False,
    )
```

time: 168 us -> 74.2 us (0.44)
  blocking collectives: 78.2 us -> 0 us
  Pallas kernels: 0 us -> 61.6 us
  waiting for transfers between devices: 26.1 us -> 0 us
  other arithmetic: 25.9 us -> 0.67 us
  matrix products: 19.2 us -> 0 us
  between operations: 17.2 us -> 0.65 us
  local copies, waits for them, and re-layouts: 1.12 us -> 10.8 us
    pallas_call x0 -> x1, Pallas kernels: none -> 61.6 us  [on_device(): pl.pallas_call(functools.partial(kernel, nf, nm), out_shape=jax.ShapeDtyp...]
    psum x2 -> x0, blocking collectives: 47 us -> none  [the longest x1 32.7 us: on_device(): lax.psum((jnp.sum(jnp.exp(capped), axis=1), jnp.sum(jnp.where(hits, cappe...]
    mul x2 -> x0, other arithmetic: 21.4 us -> none  [the longest x1 17.8 us: dequant_down(): grouped = codes.reshape(scales.shape[0], -1, cols) * scales[:, None, :]]
    dot_general x2 -> x0, matrix products: 19.2 us -> none  [the longest x1 15.8 us: on_device(): jnp.dot(lax.all_gather(hidden, 'fsdp', axis=0, tiled=True), local_weight,...]
    all_gather x1 -> x0, waiting for transfers between devices: 16.6 us -> none  [on_device(): lax.all_gather(hidden, 'fsdp', axis=0, tiled=True)]
    all_gather x1 -> x0, blocking collectives: 15.1 us -> none  [on_device(): lax.all_gather(states, ('fsdp', 'sub'), axis=0, tiled=True)]
    all_to_all x1 -> x0, blocking collectives: 9.71 us -> none  [on_device(): lax.all_to_all(partial_cols, 'fsdp', split_axis=0, concat_axis=1, tiled=T...]
    psum x1 -> x0, waiting for transfers between devices: 8.84 us -> none  [normalize_rows(): ffn = lax.psum(ffn, 'mp')]
  transfers between devices with their start and end apart: 2 -> 0, of which waited for: 2 -> 0; matrix products, arithmetic and copies ran while one was open for 13% -> 0% of each run, Pallas kernels for 0% -> 0%
where the time goes in v1:
time: 74.2 us; the launch traced here: 73.8 us
  Pallas kernels  61.6 us (83%)
  local copies, waits for them, and re-layouts  10.8 us (15%)
    pallas_call x1, Pallas kernels, on_device(): pl.pallas_call(functools.partial(kernel, nf, nm), out_shape=jax.ShapeDtyp...  61.6 us
    unnamed x2, local copies, waits for them, and re-layouts  4.28 us
    slice x2, local copies, waits for them, and re-layouts, on_device(): return (lax.dynamic_slice(table[0], (start,), (tok,)), table[1, 0:1])  1.86 us

profile of v1, /device:TPU:0, one launch (start us, length us, event | category | flops | bytes accessed | tf_op | source)
XLA Modules:
  0.0 73.8 jit_solution(11492580052034864760)
XLA Ops:
  0.6 0.7 broadcast_in_dim.20
  1.4 0.7 broadcast_in_dim.21
  2.1 0.7 pad_add_fusion.info
  2.8 1.3 %broadcast_in_dim.8.post_gain = f32[1,4608]{1,0:T(1,128)} reshape(f32[4608]{0:T(1024)} %param.14) | data formatting | bytes 36864 | tf_op jit(solution)/shard_map/broadcast_in_dim | solution.py:421
  4.1 1.3 %broadcast_in_dim.9.final_gain = f32[1,4608]{1,0:T(1,128)} reshape(f32[4608]{0:T(1024)} %param.15) | data formatting | bytes 36864 | tf_op jit(solution)/shard_map/broadcast_in_dim | solution.py:421
  5.4 1.5 %copy.13.embed_scale = bf16[512,36]{1,0:T(8,128)(2,1)} copy(bf16[512,36]{0,1:T(8,128)(2,1)} %param.17) | data formatting | bytes 73728 | tf_op args[7]
  7.0 2.7 %copy.12.embed_hbm = s32[512,576]{1,0:T(8,128)} copy(s32[512,576]{0,1:T(8,128)} %param.16) | data formatting | bytes 2359296 | tf_op args[6]
  9.7 61.6 %shard_map.113 = f32[8,128]{1,0:T(8,128)} custom-call(bf16[8,18432]{1,0:T(8,128)(2,1)} %hidden.1, bf16[8,4608]{1,0:T(8,128)(2,1)} %residual.1, s32[2304,1152]{1,0:T(8,128)} %words_hbm.1, bf16[144,1152]{1,0:T(8,128)(2,1)} %scale.1, f32[1,4608]{1,0:T(1,128)} %broadcast_in_dim.8.post_gain, f32[1,4608]{1,0:T(1,128)} %broadcast_in_dim.9.final_gain, ...), custom_call_target="tpu_custom_call" | custom-call | tf_op jit(solution)/shard_map/pallas_call | solution.py:383
  71.3 1.2 %slice.7 = f32[1,1]{1,0:T(1,128)} slice(f32[8,128]{1,0:T(8,128)} %shard_map.113), slice={[1:2], [0:1]} | slice | bytes 8 | tf_op jit(solution)/shard_map/slice | solution.py:425
  72.5 0.7 slice.6
  73.2 0.6 dynamic-slice_bitcast_fusion

commit v2 on v1

--- a/solution.py
+++ b/solution.py
@@ -26,9 +26,9 @@
 
 
 def kernel(
-    nf, nm, hidden, residual, words_hbm, scale, post_gain, final_gain, embed_hbm, embed_scale, info,
-    out, words, scale_f, weight, perm, pair, gathered, own_acc, acc_in, mid, mid_in, red, cols_in,
-    embed_words, embed, states, infos, sums,
+    nf, nm, hidden, residual, words_hbm, scale, post_gain, final_gain, embed_hbm, embed_scale, targets, mask,
+    out, mean_out, words, scale_f, weight, perm, pair, gathered, own_acc, acc_in, mid, mid_in, red, cols_in,
+    embed_words, embed_f, embed, states, info, infos, sums,
     local_sem, pair_send, pair_recv, ring_send, ring_recv, info_send, info_recv,
     acc_sem, mid_send, mid_recv, col_send, col_recv, st_send, st_recv, fwd_send, fwd_recv,
     sum_send, sum_recv,
@@ -74,7 +74,14 @@
     lax.fori_loop(0, width // step_rows, build, 0)
     scale_f[...] = scale[...].astype(jnp.float32)
     pair[s] = hidden[:, pl.ds(pl.multiple_of(s * half_k, 128), half_k)]
-    infos[me] = info[...]
+    embed_f[...] = embed_scale[...].astype(jnp.float32)
+    token = lax.broadcasted_iota(jnp.int32, (tok, 128), 0)
+    side = lax.broadcasted_iota(jnp.int32, (tok, 128), 1)
+    entry = jnp.zeros((tok, 128), jnp.int32)
+    for i in range(tok):
+        entry = jnp.where(token == i, jnp.where(side < 64, targets[i], mask[i]), entry)
+    info[...] = entry
+    infos[me] = entry
 
     pl.semaphore_wait(barrier, n - 1)
 
@@ -168,33 +175,22 @@
     lax.fori_loop(early, groups, dequant, 0)
 
     load_embed.wait()
-    vocab, packed = embed_words.shape
-    erows = 32
-    tiles = 2 * packed // 128
+    packed, vocab = embed_words.shape
+    span = packed * PLANES // embed_f.shape[0]
+    step = 32
+    blocks = packed // step
 
     def dequant_embed(i, carry):
-        start = pl.multiple_of(i * erows, erows)
-        w = embed_words[pl.ds(start, erows), :]
-        side = jnp.concatenate([w, w], axis=1)
-        es = embed_scale[pl.ds(start, erows), :].astype(jnp.float32)
-        lane = lax.broadcasted_iota(jnp.int32, (erows, 128), 1)
-        for kk in range(PLANES // 2):
-            for t in range(tiles):
-                x = side[:, t * 128:(t + 1) * 128]
-                a = 28 - 8 * kk
-                if (t + 1) * 128 <= packed:
-                    x = jnp.left_shift(x, a)
-                elif t * 128 >= packed:
-                    x = jnp.left_shift(x, a - 4)
-                else:
-                    x = jnp.left_shift(x, jnp.where(lane < packed - t * 128, a, a - 4))
-                g = kk * tiles + t
-                embed[pl.ds(start, erows), g * 128:(g + 1) * 128] = (
-                    jnp.right_shift(x, 28).astype(jnp.float32) * es[:, g:g + 1]
-                ).astype(jnp.bfloat16)
+        w = embed_words[pl.ds(pl.multiple_of(i * step, step), step), :]
+        for k in range(PLANES):
+            code = jnp.right_shift(jnp.left_shift(w, 28 - 4 * k), 28) if k < 7 else jnp.right_shift(w, 28)
+            sc = embed_f[pl.ds((k * packed + i * step) // span, 1), :]
+            embed[pl.ds(pl.multiple_of(k * packed + i * step, step), step), :] = (
+                code.astype(jnp.float32) * sc
+            ).astype(jnp.bfloat16)
         return carry
 
-    lax.fori_loop(0, vocab // erows, dequant_embed, 0)
+    lax.fori_loop(0, blocks, dequant_embed, 0)
 
     acc = jnp.zeros((total, cols), jnp.float32)
     for p in (0, 4, 1, 5, 2, 6, 3, 7):
@@ -267,9 +263,9 @@
             ).wait_recv()
         ffn = jnp.concatenate([cols_in[b] for b in range(nf)], axis=1)
         inv = lax.rsqrt(jnp.sum(ffn * ffn, axis=1, keepdims=True) / width_d + EPS)
-        stream = residual[...].astype(jnp.float32) + ffn * inv * post_gain[...]
+        stream = residual[...].astype(jnp.float32) + ffn * inv * post_gain[...].reshape(1, width_d)
         inv2 = lax.rsqrt(jnp.sum(stream * stream, axis=1, keepdims=True) / width_d + EPS)
-        states[f, s] = (stream * inv2 * final_gain[...]).astype(jnp.bfloat16)
+        states[f, s] = (stream * inv2 * final_gain[...].reshape(1, width_d)).astype(jnp.bfloat16)
         for copy in state_sends():
             copy.start()
 
@@ -304,7 +300,7 @@
 
     all_states = states[...].astype(jnp.float32).reshape(total, width_d).astype(jnp.bfloat16)
     logits = lax.dot_general(
-        all_states, embed[...], (((1,), (1,)), ((), ())), preferred_element_type=jnp.float32
+        all_states, embed[...], (((1,), (0,)), ((), ())), preferred_element_type=jnp.float32
     )
     capped = CAP * jnp.tanh(logits / CAP)
     rows = jnp.concatenate(
@@ -340,8 +336,9 @@
     mean = jnp.sum(losses, axis=1, keepdims=True) / jnp.maximum(
         jnp.sum(weights, axis=1, keepdims=True), 1.0
     )
-    row = lax.broadcasted_iota(jnp.int32, (8, pad), 0)
-    out[...] = jnp.where(row == 0, losses, mean)
+    start = (f * 2 + s) * tok
+    out[...] = pltpu.roll(losses, lax.rem(pad - start, pad), 1)[0, 0:tok]
+    mean_out[...] = mean[0]
 
     swap.wait_send()
     swap_acc.wait_send()
@@ -372,19 +369,16 @@
     total = tok * 2 * nf
     pad = -(-total // 128) * 128
     chunk = PLANES * (128 if half % 128 == 0 else half)
-    info = jnp.concatenate(
-        [jnp.broadcast_to(targets[:, None], (tok, 64)), jnp.broadcast_to(loss_mask[:, None], (tok, 64))],
-        axis=1,
-    )
     vm = pl.BlockSpec(memory_space=pltpu.VMEM)
     hbm = pl.BlockSpec(memory_space=pl.ANY)
+    sm = pl.BlockSpec(memory_space=pltpu.SMEM)
     dma = pltpu.SemaphoreType.DMA
     bf16, f32, i32 = jnp.bfloat16, jnp.float32, jnp.int32
-    table = pl.pallas_call(
+    return pl.pallas_call(
         functools.partial(kernel, nf, nm),
-        out_shape=jax.ShapeDtypeStruct((8, pad), f32),
-        in_specs=[vm, vm, hbm, vm, vm, vm, hbm, vm, vm],
-        out_specs=vm,
+        out_shape=(jax.ShapeDtypeStruct((tok,), f32), jax.ShapeDtypeStruct((1,), f32)),
+        in_specs=[vm, vm, hbm, vm, vm, vm, hbm, vm, sm, sm],
+        out_specs=(vm, vm),
         scratch_shapes=[
             pltpu.VMEM((half, cols), i32),
             pltpu.VMEM(down_scale.shape, f32),
@@ -398,9 +392,11 @@
             pltpu.VMEM((nm, nf // nm, tok, cols), f32),
             pltpu.VMEM((nf // nm, tok, cols), f32),
             pltpu.VMEM((nf, tok, cols), f32),
-            pltpu.VMEM((vocab, packed), i32),
-            pltpu.VMEM((vocab, width_d), bf16),
+            pltpu.VMEM((packed, vocab), i32),
+            pltpu.VMEM((embed_scale.shape[1], vocab), f32),
+            pltpu.VMEM((width_d, vocab), bf16),
             pltpu.VMEM((nf, 2, tok, width_d), bf16),
+            pltpu.VMEM((tok, 128), i32),
             pltpu.VMEM((n, tok, 128), i32),
             pltpu.VMEM((n, 8, pad), f32),
             dma((2,)),
@@ -418,11 +414,9 @@
             collective_id=0, has_side_effects=True, vmem_limit_bytes=62 * 1024 * 1024
         ),
     )(
-        hidden, residual, down_packed, down_scale, post_gain[None, :], final_gain[None, :],
-        embed_packed, embed_scale, info,
-    )
-    start = (lax.axis_index("fsdp") * 2 + lax.axis_index("sub")) * tok
-    return lax.dynamic_slice(table[0], (start,), (tok,)), table[1, 0:1]
+        hidden, residual, down_packed, down_scale, post_gain, final_gain,
+        embed_packed.T, embed_scale.T, targets, loss_mask,
+    )
 
 
 def solution(mesh):

time: 74.2 us -> 64.7 us (0.87)
  local copies, waits for them, and re-layouts: 10.8 us -> 1.11 us
  between operations: 0.65 us -> 2.41 us
    broadcast_in_dim x4 -> x0, local copies, waits for them, and re-layouts: 4.12 us -> none  [the longest x1 1.34 us: on_device(): post_gain[None, :]]
    unnamed x2 -> x1, local copies, waits for them, and re-layouts: 4.28 us -> 1.11 us
    slice x2 -> x0, local copies, waits for them, and re-layouts: 1.86 us -> none  [on_device(): return (lax.dynamic_slice(table[0], (start,), (tok,)), table[1, 0:1])]
where the time goes in v2:
time: 64.7 us; the launch traced here: 64.5 us
  Pallas kernels  61 us (94%)
  between operations  2.41 us (4%)
  local copies, waits for them, and re-layouts  1.11 us (2%)
    pallas_call x1, Pallas kernels, on_device(): pl.pallas_call(functools.partial(kernel, nf, nm), out_shape=(jax.ShapeDty...  61 us

profile of v2, /device:TPU:0, one launch (start us, length us, event | category | flops | bytes accessed | tf_op | source)
XLA Modules:
  0.0 64.5 jit_solution(14996686123344127157)
XLA Ops:
  0.6 61.0 %shard_map.113 = (f32[8]{0:T(128)}, f32[1]{0:T(128)}) custom-call(bf16[8,18432]{1,0:T(8,128)(2,1)} %hidden.1, bf16[8,4608]{1,0:T(8,128)(2,1)} %residual.1, s32[2304,1152]{1,0:T(8,128)} %words_hbm.1, bf16[144,1152]{1,0:T(8,128)(2,1)} %scale.1, f32[4608]{0:T(1024)} %post_gain.1, f32[4608]{0:T(1024)} %final_gain.1, s32[576,512]{1,0:T(8,128)} %bitcast.2, ...), custom_call_target="tpu_custom_call" | custom-call | tf_op jit(solution)/shard_map/pallas_call | solution.py:377
  61.6 1.1 %copy.14 = f32[8]{0:T(128)} copy(f32[8]{0:T(128)} %get-tuple-element.4) | data formatting | bytes 64

commit v3 on v2

--- a/solution.py
+++ b/solution.py
@@ -27,10 +27,10 @@
 
 def kernel(
     nf, nm, hidden, residual, words_hbm, scale, post_gain, final_gain, embed_hbm, embed_scale, targets, mask,
-    out, mean_out, words, scale_f, weight, perm, pair, gathered, own_acc, acc_in, mid, mid_in, red, cols_in,
+    out, mean_out, words, scale_f, weight, perm, sorted_own, gathered, own_acc, acc_in, mid, mid_in, red, cols_in,
     embed_words, embed_f, embed, states, info, infos, sums,
-    local_sem, pair_send, pair_recv, ring_send, ring_recv, info_send, info_recv,
-    acc_sem, mid_send, mid_recv, col_send, col_recv, st_send, st_recv, fwd_send, fwd_recv,
+    local_sem, pair_send, pair_recv, first_send, ring_send, ring_recv, info_send, info_recv,
+    acc_sem, mid_send, mid_recv, col_send, col_recv, st_send, st_recv, side_send, fwd_send, fwd_recv,
     sum_send, sum_recv,
 ):
     f, m, s = lax.axis_index("fsdp"), lax.axis_index("mp"), lax.axis_index("sub")
@@ -62,18 +62,32 @@
     q = width // PLANES
     step_rows = 128 if width % 128 == 0 else width
 
+    col = lax.broadcasted_iota(jnp.int32, (1, width), 1)
+    plane = sum(((col >= q * k).astype(jnp.int32) for k in range(1, PLANES)), jnp.zeros_like(col))
+    source = (col - plane * q) * PLANES + plane
+
     def build(i, carry):
         start = pl.multiple_of(i * step_rows, step_rows)
-        row = lax.broadcasted_iota(jnp.int32, (step_rows, width), 0) + start
-        col = lax.broadcasted_iota(jnp.int32, (step_rows, width), 1)
-        plane = sum(((col >= q * k).astype(jnp.int32) for k in range(1, PLANES)), jnp.zeros_like(col))
-        source = (col - plane * q) * PLANES + plane
-        perm[pl.ds(start, step_rows), :] = jnp.where(row == source, 1.0, 0.0).astype(jnp.bfloat16)
+        row = lax.broadcasted_iota(jnp.int32, (step_rows, width), 0)
+        perm[pl.ds(start, step_rows), :] = jnp.where(row == source - start, 1.0, 0.0).astype(
+            jnp.bfloat16
+        )
         return carry
 
     lax.fori_loop(0, width // step_rows, build, 0)
     scale_f[...] = scale[...].astype(jnp.float32)
-    pair[s] = hidden[:, pl.ds(pl.multiple_of(s * half_k, 128), half_k)]
+    own = hidden[...].astype(jnp.float32)
+    chunks = half_k // width
+    stacked = jnp.concatenate(
+        [own[:, c * width:(c + 1) * width] for c in range(2 * chunks)], axis=0
+    ).astype(jnp.bfloat16)
+    ordered = jnp.dot(stacked, perm[...], preferred_element_type=jnp.float32)
+    for c in range(2 * chunks):
+        at = (c % chunks) * q
+        for k in range(PLANES):
+            sorted_own[c // chunks, k, :, at:at + q] = ordered[
+                c * tok:(c + 1) * tok, k * q:(k + 1) * q
+            ].astype(jnp.bfloat16)
     embed_f[...] = embed_scale[...].astype(jnp.float32)
     token = lax.broadcasted_iota(jnp.int32, (tok, 128), 0)
     side = lax.broadcasted_iota(jnp.int32, (tok, 128), 1)
@@ -82,27 +96,9 @@
         entry = jnp.where(token == i, jnp.where(side < 64, targets[i], mask[i]), entry)
     info[...] = entry
     infos[me] = entry
+    gathered[f, :, s] = sorted_own[s]
 
     pl.semaphore_wait(barrier, n - 1)
-
-    swap = remote(
-        hidden.at[:, pl.ds(pl.multiple_of((1 - s) * half_k, 128), half_k)],
-        pair.at[s], pair_send, pair_recv, f, m, 1 - s,
-    )
-    swap.start()
-    swap.wait_recv()
-
-    both = pair[...].astype(jnp.float32).reshape(2 * tok, half_k)
-    chunks = half_k // width
-    stacked = jnp.concatenate(
-        [both[:, c * width:(c + 1) * width] for c in range(chunks)], axis=0
-    ).astype(jnp.bfloat16)
-    ordered = jnp.dot(stacked, perm[...], preferred_element_type=jnp.float32).astype(jnp.bfloat16)
-    for c in range(chunks):
-        for k in range(PLANES):
-            gathered[f, k, :, c * q:(c + 1) * q] = ordered[
-                c * 2 * tok:(c + 1) * 2 * tok, k * q:(k + 1) * q
-            ]
 
     far = nf // 2
     low, high = list(range(4)), list(range(4, 8))
@@ -119,11 +115,20 @@
         target = lax.rem(f + 1, nf) if way == 0 else lax.rem(f + nf - 1, nf)
         return remote(
             gathered.at[slot, p], gathered.at[slot, p], ring_send.at[way, j - 1, p],
-            ring_recv.at[slot, p], target, m, s,
+            ring_recv.at[slot, p, 0], target, m, s,
         )
 
     def send_hop(way, j, p):
-        if j < far or p in last[way]:
+        if j == 1 and (j < far or p in last[way]):
+            target = lax.rem(f + 1, nf) if way == 0 else lax.rem(f + nf - 1, nf)
+            for h in (0, 1):
+                copy = remote(
+                    sorted_own.at[h, p], gathered.at[f, p, s], first_send.at[way, p, h],
+                    ring_recv.at[f, p, s], target, m, h,
+                )
+                copy.start()
+                pending.append(copy)
+        elif j < far or p in last[way]:
             copy = hop(way, j, p)
             copy.start()
             pending.append(copy)
@@ -133,16 +138,27 @@
             return
         waited.add((way, j, p))
         slot = block_at(way, j)
-        remote(
-            gathered.at[slot, p], gathered.at[slot, p], ring_send.at[way, j - 1, p],
-            ring_recv.at[slot, p], f, m, 1 - s,
-        ).wait_recv()
+        if j == 1:
+            for h in (0, 1):
+                remote(
+                    sorted_own.at[h, p], gathered.at[slot, p, h], first_send.at[way, p, h],
+                    ring_recv.at[slot, p, h], f, m, 1 - s,
+                ).wait_recv()
+        else:
+            remote(
+                gathered.at[slot, p], gathered.at[slot, p], ring_send.at[way, j - 1, p],
+                ring_recv.at[slot, p, 0], f, m, 1 - s,
+            ).wait_recv()
 
     if nf > 1:
         for i in range(PLANES):
             for way in (0, 1):
                 send_hop(way, 1, orders[way][i])
 
+    swap = remote(
+        sorted_own.at[1 - s], gathered.at[f, :, s], pair_send, pair_recv, f, m, 1 - s
+    )
+    swap.start()
     for d in range(1, n):
         peer = lax.rem(me + d, n)
         pf, pm, ps = where_is(peer)
@@ -192,12 +208,27 @@
 
     lax.fori_loop(0, blocks, dequant_embed, 0)
 
+    for d in range(1, n):
+        src = lax.rem(me + n - d, n)
+        remote(
+            info, infos.at[src], info_send.at[d], info_recv.at[src], f, m, 1 - s
+        ).wait_recv()
+
+    rows = jnp.concatenate(
+        [infos[b * nm * 2 + h] for b in range(nf) for h in (0, 1)], axis=0
+    )
+    counted = jnp.broadcast_to(rows[:, 64:65].astype(jnp.float32), (total, 128))
+    weights = jnp.transpose(
+        jnp.concatenate([counted, jnp.zeros((total, 128), jnp.float32)], axis=0)
+    )[0:1, :]
+
+    swap.wait_recv()
     acc = jnp.zeros((total, cols), jnp.float32)
     for p in (0, 4, 1, 5, 2, 6, 3, 7):
         for j in range(1, far + 1):
             for way in (0, 1):
                 arrive(way, j, p)
-        lhs = gathered[:, p].reshape(total, half_rows)
+        lhs = gathered[:, p].astype(jnp.float32).reshape(total, half_rows).astype(jnp.bfloat16)
         acc = acc + jnp.dot(lhs, weight[p], preferred_element_type=jnp.float32)
 
     for b in range(nf):
@@ -242,15 +273,13 @@
     owner = lax.rem(f, nm) == m
 
     def state_sends():
-        copies = []
-        for df in range(nf):
-            for dm in range(nm):
-                if df or dm:
-                    copies.append(remote(
-                        states.at[f, s], states.at[f, s], st_send.at[df * nm + dm], st_recv.at[f],
-                        lax.rem(f + df, nf), lax.rem(m + dm, nm), s,
-                    ))
-        return copies
+        return [
+            remote(
+                states.at[f, s], states.at[f, s], st_send.at[df], st_recv.at[f],
+                lax.rem(f + df, nf), m, s,
+            )
+            for df in range(nf - 1, 0, -1)
+        ]
 
     width_d = nf * cols
 
@@ -274,50 +303,46 @@
             states.at[b, s], states.at[b, s], fwd_send.at[b], fwd_recv.at[b], f, m, 1 - s
         )
 
-    for d in range(nf):
-        b = lax.rem(f + d, nf)
-        got = remote(
-            states.at[b, s], states.at[b, s], st_send.at[0], st_recv.at[b], f, m, 1 - s
-        )
-        if d == 0:
-            @pl.when(jnp.logical_not(owner))
-            def _():
+    for dm in range(nm):
+        for j in range(nf // nm):
+            b = j * nm + lax.rem(m + dm, nm)
+            got = remote(
+                states.at[b, s], states.at[b, s], st_send.at[0], st_recv.at[b], f, m, 1 - s
+            )
+            if dm == 0:
+                @pl.when(b != f)
+                def _():
+                    got.wait_recv()
+
+                for side in range(1, nm):
+                    copy = remote(
+                        states.at[b, s], states.at[b, s], side_send.at[j, side], st_recv.at[b],
+                        f, lax.rem(m + side, nm), s,
+                    )
+                    copy.start()
+                    pending.append(copy)
+            else:
                 got.wait_recv()
-        else:
-            got.wait_recv()
-        copy = forward(b)
-        copy.start()
-        pending.append(copy)
+            copy = forward(b)
+            copy.start()
+            pending.append(copy)
     for b in range(nf):
         remote(
             states.at[b, 1 - s], states.at[b, 1 - s], fwd_send.at[b], fwd_recv.at[b], f, m, 1 - s
         ).wait_recv()
-    for d in range(1, n):
-        src = lax.rem(me + n - d, n)
-        remote(
-            info, infos.at[src], info_send.at[d], info_recv.at[src], f, m, 1 - s
-        ).wait_recv()
-
     all_states = states[...].astype(jnp.float32).reshape(total, width_d).astype(jnp.bfloat16)
     logits = lax.dot_general(
         all_states, embed[...], (((1,), (0,)), ((), ())), preferred_element_type=jnp.float32
     )
     capped = CAP * jnp.tanh(logits / CAP)
-    rows = jnp.concatenate(
-        [infos[b * nm * 2 + h] for b in range(nf) for h in (0, 1)], axis=0
-    )
     ids = me * vocab + lax.broadcasted_iota(jnp.int32, (total, vocab), 1)
     hits = rows[:, 0:1] == ids
     e = jnp.sum(jnp.exp(capped), axis=1, keepdims=True)
     t = jnp.sum(jnp.where(hits, capped, 0.0), axis=1, keepdims=True)
-    counted = rows[:, 64:65].astype(jnp.float32)
-    lane = lax.broadcasted_iota(jnp.int32, (total, 128), 1)
-    table = jnp.where(lane == 0, e, jnp.where(lane == 1, t, jnp.where(lane == 2, counted, 0.0)))
-    pad = sums.shape[2]
-    if pad > total:
-        table = jnp.concatenate([table, jnp.zeros((pad - total, 128), jnp.float32)], axis=0)
-    mine = jnp.transpose(table)[0:8, :]
-    sums[me] = mine
+    both = jnp.concatenate(
+        [jnp.broadcast_to(e, (total, 128)), jnp.broadcast_to(t, (total, 128))], axis=0
+    )
+    sums[me] = jnp.transpose(both)[0:1, :]
     for d in range(1, n):
         pf, pm, ps = where_is(lax.rem(me + d, n))
         copy = remote(sums.at[me], sums.at[me], sum_send.at[d], sum_recv.at[me], pf, pm, ps)
@@ -329,10 +354,10 @@
             sums.at[src], sums.at[src], sum_send.at[d], sum_recv.at[src], f, m, 1 - s
         ).wait_recv()
     added = jnp.sum(sums[...], axis=0)
-    weights = mine[2:3, :]
+    pad = 2 * total
     spot = lax.broadcasted_iota(jnp.int32, (1, pad), 1)
-    exp_sums = jnp.where(spot < total, added[0:1, :], 1.0)
-    losses = weights * (jnp.log(exp_sums) - added[1:2, :])
+    exp_sums = jnp.where(spot < total, added, 1.0)
+    losses = weights * (jnp.log(exp_sums) - pltpu.roll(added, total, 1))
     mean = jnp.sum(losses, axis=1, keepdims=True) / jnp.maximum(
         jnp.sum(weights, axis=1, keepdims=True), 1.0
     )
@@ -367,7 +392,6 @@
     half = rows // 2
     n = nf * nm * 2
     total = tok * 2 * nf
-    pad = -(-total // 128) * 128
     chunk = PLANES * (128 if half % 128 == 0 else half)
     vm = pl.BlockSpec(memory_space=pltpu.VMEM)
     hbm = pl.BlockSpec(memory_space=pl.ANY)
@@ -384,8 +408,8 @@
             pltpu.VMEM(down_scale.shape, f32),
             pltpu.VMEM((PLANES, half, cols), bf16),
             pltpu.VMEM((chunk, chunk), bf16),
-            pltpu.VMEM((2, tok, half * PLANES), bf16),
-            pltpu.VMEM((nf, PLANES, 2 * tok, half), bf16),
+            pltpu.VMEM((2, PLANES, tok, half), bf16),
+            pltpu.VMEM((nf, PLANES, 2, tok, half), bf16),
             pltpu.VMEM((2, nf, tok, cols), f32),
             pltpu.VMEM((nf, tok, cols), f32),
             pltpu.VMEM((nm, nf // nm, tok, cols), f32),
@@ -398,15 +422,15 @@
             pltpu.VMEM((nf, 2, tok, width_d), bf16),
             pltpu.VMEM((tok, 128), i32),
             pltpu.VMEM((n, tok, 128), i32),
-            pltpu.VMEM((n, 8, pad), f32),
+            pltpu.VMEM((n, 1, 2 * total), f32),
             dma((2,)),
             dma, dma,
-            dma((2, max(nf // 2, 1), PLANES)), dma((nf, PLANES)),
+            dma((2, PLANES, 2)), dma((2, max(nf // 2, 1), PLANES)), dma((nf, PLANES, 2)),
             dma((n,)), dma((n,)),
             dma((2,)),
             dma((nm,)), dma((nm,)),
             dma((nf // nm,)), dma((nf,)),
-            dma((nf * nm,)), dma((nf,)),
+            dma((nf,)), dma((nf,)), dma((nf // nm, nm)),
             dma((nf,)), dma((nf,)),
             dma((n,)), dma((n,)),
         ],

time: 64.7 us -> 60.3 us (0.932)
  Pallas kernels: 61 us -> 56.6 us
    pallas_call x1, Pallas kernels: 61 us -> 56.6 us  [on_device(): pl.pallas_call(functools.partial(kernel, nf, nm), out_shape=(jax.ShapeDty...]
where the time goes in v3:
time: 60.3 us; the launch traced here: 60.1 us
  Pallas kernels  56.6 us (94%)
  between operations  2.41 us (4%)
  local copies, waits for them, and re-layouts  1.11 us (2%)
    pallas_call x1, Pallas kernels, on_device(): pl.pallas_call(functools.partial(kernel, nf, nm), out_shape=(jax.ShapeDty...  56.6 us

profile of v3, /device:TPU:0, one launch (start us, length us, event | category | flops | bytes accessed | tf_op | source)
XLA Modules:
  0.0 60.1 jit_solution(12699854509848464520)
XLA Ops:
  0.6 56.6 %shard_map.113 = (f32[8]{0:T(128)}, f32[1]{0:T(128)}) custom-call(bf16[8,18432]{1,0:T(8,128)(2,1)} %hidden.1, bf16[8,4608]{1,0:T(8,128)(2,1)} %residual.1, s32[2304,1152]{1,0:T(8,128)} %words_hbm.1, bf16[144,1152]{1,0:T(8,128)(2,1)} %scale.1, f32[4608]{0:T(1024)} %post_gain.1, f32[4608]{0:T(1024)} %final_gain.1, s32[576,512]{1,0:T(8,128)} %bitcast.2, ...), custom_call_target="tpu_custom_call" | custom-call | tf_op jit(solution)/shard_map/pallas_call | solution.py:401
  57.3 1.1 %copy.14 = f32[8]{0:T(128)} copy(f32[8]{0:T(128)} %get-tuple-element.4) | data formatting | bytes 64

commit v4 on v3

--- a/solution.py
+++ b/solution.py
@@ -12,6 +12,7 @@
 MESH = pl.DeviceIdType.MESH
 PLANES = 8
 EARLY = 0.6
+PIECES = 2
 
 
 def remote(src, dst, send, recv, f, m, s):
@@ -275,9 +276,10 @@
     def state_sends():
         return [
             remote(
-                states.at[f, s], states.at[f, s], st_send.at[df], st_recv.at[f],
+                states.at[h, f, s], states.at[h, f, s], st_send.at[h, df], st_recv.at[h, f],
                 lax.rem(f + df, nf), m, s,
             )
+            for h in range(PIECES)
             for df in range(nf - 1, 0, -1)
         ]
 
@@ -294,46 +296,56 @@
         inv = lax.rsqrt(jnp.sum(ffn * ffn, axis=1, keepdims=True) / width_d + EPS)
         stream = residual[...].astype(jnp.float32) + ffn * inv * post_gain[...].reshape(1, width_d)
         inv2 = lax.rsqrt(jnp.sum(stream * stream, axis=1, keepdims=True) / width_d + EPS)
-        states[f, s] = (stream * inv2 * final_gain[...].reshape(1, width_d)).astype(jnp.bfloat16)
+        done = (stream * inv2 * final_gain[...].reshape(1, width_d)).astype(jnp.bfloat16)
+        for h in range(PIECES):
+            states[h, f, s] = done[:, h * (width_d // PIECES):(h + 1) * (width_d // PIECES)]
         for copy in state_sends():
             copy.start()
 
-    def forward(b):
+    def forward(h, b):
         return remote(
-            states.at[b, s], states.at[b, s], fwd_send.at[b], fwd_recv.at[b], f, m, 1 - s
+            states.at[h, b, s], states.at[h, b, s], fwd_send.at[h, b], fwd_recv.at[h, b],
+            f, m, 1 - s,
         )
 
     for dm in range(nm):
-        for j in range(nf // nm):
-            b = j * nm + lax.rem(m + dm, nm)
-            got = remote(
-                states.at[b, s], states.at[b, s], st_send.at[0], st_recv.at[b], f, m, 1 - s
-            )
-            if dm == 0:
-                @pl.when(b != f)
-                def _():
+        for h in range(PIECES):
+            for j in range(nf // nm):
+                b = j * nm + lax.rem(m + dm, nm)
+                got = remote(
+                    states.at[h, b, s], states.at[h, b, s], st_send.at[h, 0], st_recv.at[h, b],
+                    f, m, 1 - s,
+                )
+                if dm == 0:
+                    @pl.when(b != f)
+                    def _():
+                        got.wait_recv()
+
+                    for side in range(1, nm):
+                        copy = remote(
+                            states.at[h, b, s], states.at[h, b, s], side_send.at[h, j, side],
+                            st_recv.at[h, b], f, lax.rem(m + side, nm), s,
+                        )
+                        copy.start()
+                        pending.append(copy)
+                else:
                     got.wait_recv()
-
-                for side in range(1, nm):
-                    copy = remote(
-                        states.at[b, s], states.at[b, s], side_send.at[j, side], st_recv.at[b],
-                        f, lax.rem(m + side, nm), s,
-                    )
-                    copy.start()
-                    pending.append(copy)
-            else:
-                got.wait_recv()
-            copy = forward(b)
-            copy.start()
-            pending.append(copy)
-    for b in range(nf):
-        remote(
-            states.at[b, 1 - s], states.at[b, 1 - s], fwd_send.at[b], fwd_recv.at[b], f, m, 1 - s
-        ).wait_recv()
-    all_states = states[...].astype(jnp.float32).reshape(total, width_d).astype(jnp.bfloat16)
-    logits = lax.dot_general(
-        all_states, embed[...], (((1,), (0,)), ((), ())), preferred_element_type=jnp.float32
-    )
+                copy = forward(h, b)
+                copy.start()
+                pending.append(copy)
+    for h in range(PIECES):
+        for b in range(nf):
+            remote(
+                states.at[h, b, 1 - s], states.at[h, b, 1 - s], fwd_send.at[h, b],
+                fwd_recv.at[h, b], f, m, 1 - s,
+            ).wait_recv()
+    logits = jnp.zeros((total, vocab), jnp.float32)
+    part_d = width_d // PIECES
+    for h in range(PIECES):
+        some = states[h].astype(jnp.float32).reshape(total, part_d).astype(jnp.bfloat16)
+        logits = logits + jnp.dot(
+            some, embed[h * part_d:(h + 1) * part_d, :], preferred_element_type=jnp.float32
+        )
     capped = CAP * jnp.tanh(logits / CAP)
     ids = me * vocab + lax.broadcasted_iota(jnp.int32, (total, vocab), 1)
     hits = rows[:, 0:1] == ids
@@ -419,7 +431,7 @@
             pltpu.VMEM((packed, vocab), i32),
             pltpu.VMEM((embed_scale.shape[1], vocab), f32),
             pltpu.VMEM((width_d, vocab), bf16),
-            pltpu.VMEM((nf, 2, tok, width_d), bf16),
+            pltpu.VMEM((PIECES, nf, 2, tok, width_d // PIECES), bf16),
             pltpu.VMEM((tok, 128), i32),
             pltpu.VMEM((n, tok, 128), i32),
             pltpu.VMEM((n, 1, 2 * total), f32),
@@ -430,8 +442,8 @@
             dma((2,)),
             dma((nm,)), dma((nm,)),
             dma((nf // nm,)), dma((nf,)),
-            dma((nf,)), dma((nf,)), dma((nf // nm, nm)),
-            dma((nf,)), dma((nf,)),
+            dma((PIECES, nf)), dma((PIECES, nf)), dma((PIECES, nf // nm, nm)),
+            dma((PIECES, nf)), dma((PIECES, nf)),
             dma((n,)), dma((n,)),
         ],
         compiler_params=pltpu.CompilerParams(

time: 60.3 us -> 60.6 us (level)
  no operation moved by 1% of the time
where the time goes in v4:
time: 60.6 us; the launch traced here: 60.4 us
  Pallas kernels  56.9 us (94%)
  between operations  2.41 us (4%)
  local copies, waits for them, and re-layouts  1.11 us (2%)
    pallas_call x1, Pallas kernels, on_device(): pl.pallas_call(functools.partial(kernel, nf, nm), out_shape=(jax.ShapeDty...  56.9 us

profile of v4, /device:TPU:0, one launch (start us, length us, event | category | flops | bytes accessed | tf_op | source)
XLA Modules:
  0.0 60.4 jit_solution(9950885260525810156)
XLA Ops:
  0.6 56.9 %shard_map.113 = (f32[8]{0:T(128)}, f32[1]{0:T(128)}) custom-call(bf16[8,18432]{1,0:T(8,128)(2,1)} %hidden.1, bf16[8,4608]{1,0:T(8,128)(2,1)} %residual.1, s32[2304,1152]{1,0:T(8,128)} %words_hbm.1, bf16[144,1152]{1,0:T(8,128)(2,1)} %scale.1, f32[4608]{0:T(1024)} %post_gain.1, f32[4608]{0:T(1024)} %final_gain.1, s32[576,512]{1,0:T(8,128)} %bitcast.2, ...), custom_call_target="tpu_custom_call" | custom-call | tf_op jit(solution)/shard_map/pallas_call | solution.py:413
  57.5 1.1 %copy.14 = f32[8]{0:T(128)} copy(f32[8]{0:T(128)} %get-tuple-element.4) | data formatting | bytes 64
